TPU v7x, 32 devices: a whole 2x2x4 slice. The times are simulated.
32 devices in a mesh: dp: 8 (over y, x, core), mp: 4 (over z).
Axes of the slice: x: 2, y: 2, z: 4, core: 2. Of those that a mesh axis runs over, the one named last changes fastest.
Arguments:
- candidates: bfloat16 [64, 256, 768], P('dp', 'mp'), may hold values from -6 to 6
- owner_row: int32 [64], replicated, may hold values from 0 to 63, as said below
- selected: int32 [16], replicated, may hold values from 0 to 63, as said below
- dest_slot: int32 [16], replicated, may hold values from 0 to 15, as said below
- patch_weight: bfloat16 [768, 768], P(None, 'mp'), may hold values from -0.21875 to 0.21875
- positions: bfloat16 [256, 768], P(None, 'mp'), may hold values from -3 to 3
- qkv_weight: bfloat16 [768, 3, 768], P(None, None, 'mp'), may hold values from -1 to 1
- out_weight: bfloat16 [768, 768], P('mp'), may hold values from -0.21875 to 0.21875
- attn_gain: bfloat16 [768], replicated, may hold values from 0.099609375 to 1.8984375
- mlp_gain: bfloat16 [768], replicated, may hold values from 0.099609375 to 1.8984375
- up_weight: bfloat16 [768, 3072], P(None, 'mp'), may hold values from -0.21875 to 0.21875
- down_weight: bfloat16 [3072, 768], P('mp'), may hold values from -0.109375 to 0.109375
Outputs:
- layer_out: bfloat16 [16, 256, 768], P('dp', 'mp')
Inputs may be any that keep to these rules, and one draw needn't show every extreme that they name: `owner_row`: a permutation; storage row r sits on index r // 8 of dp. `selected`: distinct candidates; no index of dp stores more than 4 of them, and some index stores exactly 4. `dest_slot`: a permutation; the 2 slots s with equal s // 2 get candidates stored on different indices of dp.
All inputs are finite; a program needn't handle non-finite values.
Results may differ from a plain program's by a relative error of at most 0.012.
Values may be sent and summed in bfloat16 or wider, within the bound.
No kernel may reach another device: no remote copies, remote signals or barrier semaphores. Data moves between devices by JAX's collectives and lax.ppermute only.
A program may use at most 128 MiB of HBM per device.

v0:
```python
import jax
import jax.numpy as jnp
from jax import lax
from jax.sharding import PartitionSpec as P

PATCHES = 256
CAND_DEV = 8
SEL_DEV = 2
HEAD_DIM = 64


def norm_rows(values, gain):
    average = jnp.mean(values, axis=-1, keepdims=True)
    centred = values - average
    variance = jnp.mean(centred * centred, axis=-1, keepdims=True)
    return centred * lax.rsqrt(variance + 1e-06) * gain.astype(jnp.float32)


def local(
    candidates,
    owner_row,
    selected,
    dest_slot,
    patch_weight,
    positions,
    qkv_weight,
    out_weight,
    attn_gain,
    mlp_gain,
    up_weight,
    down_weight,
):
    learners = lax.axis_size("dp")
    own_index = lax.axis_index("dp")
    quarter = candidates.shape[1]
    pixel_width = candidates.shape[2]
    chosen_rows = jnp.take(owner_row, selected)
    slot_rows = jnp.zeros(dest_slot.shape, jnp.int32).at[dest_slot].set(chosen_rows)
    source_owner = slot_rows // CAND_DEV
    local_row = slot_rows % CAND_DEV
    stored = candidates.reshape(CAND_DEV, quarter * pixel_width)
    mine = (source_owner == own_index).reshape(learners, SEL_DEV)
    picked = jnp.sum(jnp.where(mine, local_row.reshape(learners, SEL_DEV), 0), axis=1)
    outgoing = jnp.take(stored, picked, axis=0)
    incoming = lax.all_to_all(outgoing, "dp", split_axis=0, concat_axis=0, tiled=True)
    senders = lax.dynamic_slice_in_dim(source_owner, own_index * SEL_DEV, SEL_DEV)
    arrived = jnp.take(incoming, senders, axis=0)
    own_pixels = arrived.reshape(SEL_DEV, quarter, pixel_width)
    product = jnp.einsum(
        "brp,pe->bre",
        lax.all_gather(own_pixels, "mp", axis=1, tiled=True),
        patch_weight,
        preferred_element_type=jnp.float32,
    )
    embedded = (product + positions.astype(jnp.float32)[None]).astype(jnp.bfloat16)
    activations = lax.all_gather(embedded, "mp", axis=2, tiled=True).astype(jnp.float32)
    normed = norm_rows(activations, attn_gain).astype(jnp.bfloat16)
    projected = jnp.einsum(
        "btd,dce->btce", normed, qkv_weight, preferred_element_type=jnp.float32
    ).astype(jnp.bfloat16)
    local_heads = qkv_weight.shape[2] // HEAD_DIM
    head_split = projected.reshape(SEL_DEV, PATCHES, 3, local_heads, HEAD_DIM)
    queries = head_split[:, :, 0]
    attn_keys = head_split[:, :, 1]
    attn_values = head_split[:, :, 2]
    scores = jnp.einsum(
        "bqhd,bkhd->bhqk", queries, attn_keys, preferred_element_type=jnp.float32
    ) * HEAD_DIM ** (-0.5)
    attn_probs = jax.nn.softmax(scores, axis=-1).astype(jnp.bfloat16)
    context = jnp.einsum(
        "bhqk,bkhd->bqhd", attn_probs, attn_values, preferred_element_type=jnp.float32
    ).astype(jnp.bfloat16)
    context = context.reshape(SEL_DEV, PATCHES, local_heads * HEAD_DIM)
    partial_out = jnp.einsum("bte,ed->btd", context, out_weight, preferred_element_type=jnp.float32)
    attended = lax.psum(partial_out.astype(jnp.bfloat16), "mp").astype(jnp.float32)
    after_attn = activations + attended
    normed2 = norm_rows(after_attn, mlp_gain).astype(jnp.bfloat16)
    hidden = jax.nn.gelu(
        jnp.einsum("btd,df->btf", normed2, up_weight, preferred_element_type=jnp.float32),
        approximate=False,
    ).astype(jnp.bfloat16)
    down_terms = jnp.einsum("btf,fd->btd", hidden, down_weight, preferred_element_type=jnp.float32)
    summed = lax.psum_scatter(
        down_terms.astype(jnp.bfloat16), "mp", scatter_dimension=1, tiled=True
    ).astype(jnp.float32)
    residual = lax.dynamic_slice_in_dim(after_attn, lax.axis_index("mp") * quarter, quarter, 1)
    return (residual + summed).astype(jnp.bfloat16)


def solution(mesh):
    return jax.shard_map(
        local,
        mesh=mesh,
        in_specs=(
            P("dp", "mp", None),
            P(),
            P(),
            P(),
            P(None, "mp"),
            P(None, "mp"),
            P(None, None, "mp"),
            P("mp", None),
            P(),
            P(),
            P(None, "mp"),
            P("mp", None),
        ),
        out_specs=P("dp", "mp", None),
        check_vma=False,
    )
```

profile of v0, /device:TPU:0, one launch (start us, length us, event | category | flops | bytes accessed | tf_op | source)
XLA Modules:
  0.0 183.8 jit_solution(13271876456663978697)
XLA Ops:
  6.5 0.8 compare_select_fusion.3
  7.3 1.3 gather_fusion
  8.6 0.7 compare_select_fusion.4
  9.3 0.6 scatter_custom_fusion
  9.9 0.1 select_n.81
  10.0 0.1 reduce_sum.56
  10.2 1.6 copy.77
  11.8 1.1 gather_fusion.1
  12.8 0.1 bitcast_select_fusion
  13.0 0.5 broadcast.218
  13.5 1.2 reduce.4
  14.7 1.5 reshape.149
  16.2 5.2 %all-to-all-start = ((bf16[8,2,24576]{2,1,0:T(2,128)(2,1)}), bf16[8,2,24576]{2,1,0:T(2,128)(2,1)S(1)}, u32[]{:S(2)}, u32[]{:S(2)}) async-start(bf16[8,2,24576]{2,1,0:T(2,128)(2,1)} %reshape.149), calls=%async_computation | async-start | bytes 1572864 | tf_op jit(solution)/shard_map/all_to_all | solution.py:45
  21.4 0.0 all-reduce.4.cloned.1.call-start
  21.5 0.7 convert_element_type.51
  22.2 0.1 compare_and_fusion.1
  22.3 11.7 %all-to-all-done = bf16[8,2,24576]{2,1,0:T(2,128)(2,1)S(1)} async-done(((bf16[8,2,24576]{2,1,0:T(2,128)(2,1)}), bf16[8,2,24576]{2,1,0:T(2,128)(2,1)S(1)}, u32[]{:S(2)}, u32[]{:S(2)}) %all-to-all-start) | async-done | bytes 786464 | tf_op jit(solution)/shard_map/all_to_all | solution.py:45
  34.0 0.8 reshape.150
  34.8 0.9 copy.82
  35.7 0.8 gather_fusion.2
  36.5 0.1 bitcast_select_fusion.1
  36.6 18.1 %all_gather.6 = bf16[2,256,768]{2,1,0:T(8,128)(2,1)S(1)} all-gather(bf16[2,64,768]{2,1,0:T(8,128)(2,1)S(1)} %bitcast_select_fusion.1), channel_id=1, replica_groups=mesh['dp'=8,'mp'=4] {'mp'}, dimensions={1}, use_global_device_ids=true | all-gather | bytes 983040 | tf_op jit(solution)/shard_map/all_gather | solution.py:51
  54.7 0.4 fusion.20
  55.1 0.2 copy.63
  55.3 17.4 %all_gather.7 = bf16[2,256,768]{1,0,2:T(2,128)(2,1)S(1)} all-gather(bf16[2,256,192]{1,0,2:T(2,128)(2,1)S(1)} %copy.63), channel_id=1, replica_groups=mesh['dp'=8,'mp'=4] {'mp'}, dimensions={2}, use_global_device_ids=true | all-gather | bytes 983040 | tf_op jit(solution)/shard_map/all_gather | solution.py:56
  72.7 0.6 copy.64
  73.3 0.2 convert_reduce_fusion
  73.5 0.4 fusion.4
  73.9 0.6 copy-done.9
  74.5 0.8 convolution_convert_fusion.2
  75.3 0.7 fusion.108
  76.0 0.9 convolution_convert_fusion.3
  76.9 0.1 copy-done.3
  76.9 1.3 convolution_convert_fusion.1
  78.3 0.0 all-reduce.4.cloned.1.call-update
  78.3 0.2 all-reduce.6.cloned.1.call-start
  78.5 44.0 %all-reduce.4.cloned.1.call-done = bf16[2,256,768]{2,1,0:T(8,128)(2,1)} async-done(((bf16[2,256,768]{2,1,0:T(8,128)(2,1)}), bf16[2,256,768]{2,1,0:T(8,128)(2,1)}) %all-reduce.4.cloned.1.call-update) | async-done | bytes 786448 | tf_op jit(solution)/shard_map/psum | solution.py:75
  122.5 1.5 fusion.107
  124.0 0.4 multiply_reduce_fusion
  124.5 1.3 fusion.63
  125.7 4.4 %convolution_convert_fusion = bf16[2,256,768]{2,1,0:T(8,128)(2,1)S(1)} fusion(bf16[768,768]{1,0:T(8,128)(2,1)S(1)} %copy-done.8, f32[2,256,768]{2,1,0:T(8,128)S(1)} %get-tuple-element.13, u8[256,768]{1,0:T(8,128)(4,1)S(1)} %get-tuple-element.6, u8[256,768]{1,0:T(8,128)(4,1)S(1)} %get-tuple-element.5), kind=kOutput, calls=%fused_computation.41 | convolution fusion | flops 631898112 | bytes 3932160 | tf_op jit(solution)/shard_map/btf,fd->btd/dot_general | solution.py:82
  130.2 0.0 copy-start.10
  130.2 1.7 copy.69
  131.9 0.0 all-reduce.6.cloned.1.call-update
  131.9 0.6 dynamic-slice
  133.2 42.0 %all-reduce.6.cloned.1.call-done = bf16[2,256,768]{2,0,1:T(2,128)(2,1)} async-done(((bf16[2,256,768]{2,0,1:T(2,128)(2,1)}), bf16[2,256,768]{2,0,1:T(2,128)(2,1)}) %all-reduce.6.cloned.1.call-update) | async-done | bytes 786448
  175.2 1.1 constant_dynamic-slice_fusion
  176.3 0.7 add_convert_fusion
  (31 shorter events, 0.1 us)
Async XLA Ops:
  6.5 117.9 %copy-start = (bf16[768,768]{1,0:T(8,128)(2,1)S(1)}, bf16[768,768]{1,0:T(8,128)(2,1)}, u32[]{:S(2)}) copy-start(bf16[768,768]{1,0:T(8,128)(2,1)} %param.22) | copy-start | bytes 3538948
  14.7 6.8 %copy-start.5 = (bf16[256,192]{0,1:T(8,128)(2,1)S(1)}, bf16[256,192]{0,1:T(8,128)(2,1)}, u32[]{:S(2)}) copy-start(bf16[256,192]{0,1:T(8,128)(2,1)} %param.17) | copy-start | bytes 294916
  14.7 7.5 %copy-start.6 = (bf16[768]{0:T(1024)(128)(2,1)S(1)}, bf16[768]{0:T(1024)(128)(2,1)}, u32[]{:S(2)}) copy-start(bf16[768]{0:T(1024)(128)(2,1)} %param.20) | copy-start | bytes 4612
  16.2 17.8 %all-to-all-start = ((bf16[8,2,24576]{2,1,0:T(2,128)(2,1)}), bf16[8,2,24576]{2,1,0:T(2,128)(2,1)S(1)}, u32[]{:S(2)}, u32[]{:S(2)}) async-start(bf16[8,2,24576]{2,1,0:T(2,128)(2,1)} %reshape.149), calls=%async_computation | async-start | bytes 1572864 | tf_op jit(solution)/shard_map/all_to_all | solution.py:45
  21.4 101.1 %all-reduce.4.cloned.1.call-start = ((), (), s32[]{:S(2)}) async-start(), calls=%async_computation.1 | async-start | bytes 1572864 | tf_op jit(solution)/shard_map/psum | solution.py:75
  35.7 19.0 %copy-start.2 = (f32[256,192]{0,1:T(8,128)S(1)}, f32[256,192]{0,1:T(8,128)}, u32[]{:S(2)}) copy-start(f32[256,192]{0,1:T(8,128)} %convert_element_type.51) | copy-start | bytes 589828
  35.7 19.0 %copy-start.4 = (bf16[768,192]{0,1:T(8,128)(2,1)S(1)}, bf16[768,192]{0,1:T(8,128)(2,1)}, u32[]{:S(2)}) copy-start(bf16[768,192]{0,1:T(8,128)(2,1)} %param.16) | copy-start | bytes 884740
  73.3 1.2 copy-start.9
  76.0 1.0 copy-start.3
  76.9 1.6 copy-start.7
  78.3 96.9 %all-reduce.6.cloned.1.call-start = ((), (), s32[]{:S(2)}) async-start(), calls=%async_computation.2 | async-start | bytes 1572864
  122.5 1.5 copy-start.1
  124.4 1.3 copy-start.8
  130.2 1.8 copy-start.10
Sparse Core Ops, SparseCore 0:
  78.4 44.0 all-reduce.3
  132.0 43.1 all-reduce.5
where the time goes:
time: 184 us
  waiting for transfers between devices  97.8 us (53%)
  blocking collectives  35.5 us (19%)
  between operations  14.3 us (8%)
  local copies, waits for them, and re-layouts  14 us (8%)
  matrix products  9.79 us (5%)
  other arithmetic  7.02 us (4%)
  starting transfers between devices  5.46 us (3%)
    psum x1, waiting for transfers between devices, local(): lax.psum(partial_out.astype(jnp.bfloat16), 'mp').astype(jnp.float32)  44 us
    unnamed x3, waiting for transfers between devices  42.1 us
    all_gather x1, blocking collectives, local(): lax.all_gather(own_pixels, 'mp', axis=1, tiled=True)  18.1 us
    all_gather x1, blocking collectives, local(): lax.all_gather(embedded, 'mp', axis=2, tiled=True).astype(jnp.float32)  17.4 us
    all_to_all x1, waiting for transfers between devices, local(): lax.all_to_all(outgoing, 'dp', split_axis=0, concat_axis=0, tiled=True)  11.7 us
    unnamed x28, local copies, waits for them, and re-layouts  7.11 us
    all_to_all x1, starting transfers between devices, local(): lax.all_to_all(outgoing, 'dp', split_axis=0, concat_axis=0, tiled=True)  5.2 us
    dot_general x1, matrix products, local(): jnp.einsum('btf,fd->btd', hidden, down_weight, preferred_element_type=jnp...  4.43 us
  transfers between devices with their start and end apart: 3, of which 3 were waited for; matrix products, arithmetic and copies ran while one was open for 1% of the time, Pallas kernels for 0%

commit v1 on v0

--- a/solution.py
+++ b/solution.py
@@ -2,11 +2,16 @@
 import jax.numpy as jnp
 from jax import lax
 from jax.sharding import PartitionSpec as P
+from jax.lax import all_gather
 
 PATCHES = 256
 CAND_DEV = 8
 SEL_DEV = 2
 HEAD_DIM = 64
+
+
+def lift_digits(x_in, group_axis):
+    return jnp.sum(all_gather(x_in, axis_name=group_axis), 0)
 
 
 def norm_rows(values, gain):
@@ -72,7 +77,7 @@
     ).astype(jnp.bfloat16)
     context = context.reshape(SEL_DEV, PATCHES, local_heads * HEAD_DIM)
     partial_out = jnp.einsum("bte,ed->btd", context, out_weight, preferred_element_type=jnp.float32)
-    attended = lax.psum(partial_out.astype(jnp.bfloat16), "mp").astype(jnp.float32)
+    attended = lift_digits(partial_out.astype(jnp.bfloat16), "mp").astype(jnp.float32)
     after_attn = activations + attended
     normed2 = norm_rows(after_attn, mlp_gain).astype(jnp.bfloat16)
     hidden = jax.nn.gelu(

time: 184 us -> 207 us (1.12)
  waiting for transfers between devices: 97.8 us -> 117 us
  other arithmetic: 7.02 us -> 10.5 us
    all_gather x0 -> x1, waiting for transfers between devices: none -> 63.5 us  [lift_digits(): return jnp.sum(all_gather(x_in, axis_name=group_axis), 0)]
    psum x1 -> x0, waiting for transfers between devices: 44 us -> none  [local(): lax.psum(partial_out.astype(jnp.bfloat16), 'mp').astype(jnp.float32)]
    reduce_sum x0 -> x1, other arithmetic: none -> 2.6 us  [lift_digits(): return jnp.sum(all_gather(x_in, axis_name=group_axis), 0)]
    unnamed x28 -> x26, local copies, waits for them, and re-layouts: 7.11 us -> 7.12 us
where the time goes in v1:
time: 207 us; the launch traced here: 206 us
  waiting for transfers between devices  117 us (57%)
  blocking collectives  35.5 us (17%)
  between operations  14.3 us (7%)
  local copies, waits for them, and re-layouts  14 us (7%)
  other arithmetic  10.5 us (5%)
  matrix products  9.72 us (5%)
  starting transfers between devices  5.46 us (3%)
    all_gather x1, waiting for transfers between devices, lift_digits(): return jnp.sum(all_gather(x_in, axis_name=group_axis), 0)  63.5 us
    unnamed x3, waiting for transfers between devices  41.4 us
    all_gather x1, blocking collectives, local(): lax.all_gather(own_pixels, 'mp', axis=1, tiled=True)  18.1 us
    all_gather x1, blocking collectives, local(): lax.all_gather(embedded, 'mp', axis=2, tiled=True).astype(jnp.float32)  17.4 us
    all_to_all x1, waiting for transfers between devices, local(): lax.all_to_all(outgoing, 'dp', split_axis=0, concat_axis=0, tiled=True)  11.7 us
    unnamed x26, local copies, waits for them, and re-layouts  7.12 us
    all_to_all x1, starting transfers between devices, local(): lax.all_to_all(outgoing, 'dp', split_axis=0, concat_axis=0, tiled=True)  5.2 us
    dot_general x1, matrix products, local(): jnp.einsum('btf,fd->btd', hidden, down_weight, preferred_element_type=jnp...  4.41 us
  transfers between devices with their start and end apart: 3, of which 3 were waited for; matrix products, arithmetic and copies ran while one was open for 1% of the time, Pallas kernels for 0%

profile of v1, /device:TPU:0, one launch (start us, length us, event | category | flops | bytes accessed | tf_op | source)
XLA Modules:
  0.0 206.1 jit_solution(14278742000363332639)
XLA Ops:
  6.5 0.8 compare_select_fusion.3
  7.3 1.3 gather_fusion
  8.6 0.7 compare_select_fusion.4
  9.3 0.6 scatter_custom_fusion
  9.9 0.1 select_n.81
  10.0 0.1 reduce_sum.68
  10.2 1.6 copy.75
  11.8 1.1 gather_fusion.1
  12.8 0.1 bitcast_select_fusion
  13.0 0.5 broadcast.218
  13.5 1.2 reduce.5
  14.7 1.5 reshape.150
  16.2 5.2 %all-to-all-start = ((bf16[8,2,24576]{2,1,0:T(2,128)(2,1)}), bf16[8,2,24576]{2,1,0:T(2,128)(2,1)S(1)}, u32[]{:S(2)}, u32[]{:S(2)}) async-start(bf16[8,2,24576]{2,1,0:T(2,128)(2,1)} %reshape.150), calls=%async_computation | async-start | bytes 1572864 | tf_op jit(solution)/shard_map/all_to_all | solution.py:50
  21.4 0.0 all-gather.3.cloned.1.call-start
  21.5 0.7 convert_element_type.53
  22.2 0.1 compare_and_fusion.1
  22.3 11.7 %all-to-all-done = bf16[8,2,24576]{2,1,0:T(2,128)(2,1)S(1)} async-done(((bf16[8,2,24576]{2,1,0:T(2,128)(2,1)}), bf16[8,2,24576]{2,1,0:T(2,128)(2,1)S(1)}, u32[]{:S(2)}, u32[]{:S(2)}) %all-to-all-start) | async-done | bytes 786464 | tf_op jit(solution)/shard_map/all_to_all | solution.py:50
  34.0 0.8 reshape.151
  34.8 0.9 copy.80
  35.7 0.8 gather_fusion.2
  36.5 0.1 bitcast_select_fusion.1
  36.6 18.1 %all_gather.12 = bf16[2,256,768]{2,1,0:T(8,128)(2,1)S(1)} all-gather(bf16[2,64,768]{2,1,0:T(8,128)(2,1)S(1)} %bitcast_select_fusion.1), channel_id=1, replica_groups=mesh['dp'=8,'mp'=4] {'mp'}, dimensions={1}, use_global_device_ids=true | all-gather | bytes 983040 | tf_op jit(solution)/shard_map/all_gather | solution.py:56
  54.7 0.4 fusion.20
  55.1 0.2 copy.61
  55.3 17.4 %all_gather.13 = bf16[2,256,768]{1,0,2:T(2,128)(2,1)S(1)} all-gather(bf16[2,256,192]{1,0,2:T(2,128)(2,1)S(1)} %copy.61), channel_id=1, replica_groups=mesh['dp'=8,'mp'=4] {'mp'}, dimensions={2}, use_global_device_ids=true | all-gather | bytes 983040 | tf_op jit(solution)/shard_map/all_gather | solution.py:61
  72.7 0.6 copy.62
  73.3 0.2 convert_reduce_fusion
  73.5 0.4 fusion.4
  73.9 0.6 copy-done.8
  74.5 0.8 convolution_convert_fusion.2
  75.3 0.7 fusion.108
  76.0 0.9 convolution_convert_fusion.3
  76.9 0.1 copy-done.2
  76.9 1.3 convolution_convert_fusion.1
  78.2 0.0 all-gather.3.cloned.1.call-update
  78.3 0.2 all-reduce.3.cloned.1.call-start
  78.5 63.5 %all-gather.3.cloned.1.call-done = bf16[8,256,768]{2,1,0:T(8,128)(2,1)} async-done(((bf16[2,256,768]{2,1,0:T(8,128)(2,1)}), bf16[8,256,768]{2,1,0:T(8,128)(2,1)}) %all-gather.3.cloned.1.call-update) | async-done | bytes 3145744 | tf_op jit(solution)/shard_map/all_gather | solution.py:14
  142.0 2.6 %reduce_sum.73 = bf16[2,256,768]{2,1,0:T(8,128)(2,1)S(1)} reduce(bf16[4,2,256,768]{3,2,1,0:T(8,128)(2,1)} %bitcast.81, bf16[]{:T(256)} %constant.72.clone.1), dimensions={0}, to_apply=%region_6.7 | reduce | flops 1179648 | bytes 3932162 | tf_op jit(solution)/shard_map/reduce_sum | solution.py:14
  144.6 0.3 fusion.107
  144.9 1.5 multiply_reduce_fusion
  146.4 1.2 fusion.63
  147.7 0.0 copy-done.7
  147.7 4.4 %convolution_convert_fusion = bf16[2,256,768]{2,1,0:T(8,128)(2,1)S(1)} fusion(bf16[768,768]{1,0:T(8,128)(2,1)S(1)} %copy-done.7, f32[2,256,768]{2,1,0:T(8,128)S(1)} %get-tuple-element.13, u8[256,768]{1,0:T(8,128)(4,1)S(1)} %get-tuple-element.6, u8[256,768]{1,0:T(8,128)(4,1)S(1)} %get-tuple-element.5), kind=kOutput, calls=%fused_computation.41 | convolution fusion | flops 631898112 | bytes 3932160 | tf_op jit(solution)/shard_map/btf,fd->btd/dot_general | solution.py:87
  152.1 1.7 copy.67
  153.9 0.6 dynamic-slice
  155.1 41.4 %all-reduce.3.cloned.1.call-done = bf16[2,256,768]{2,0,1:T(2,128)(2,1)} async-done(((bf16[2,256,768]{2,0,1:T(2,128)(2,1)}), bf16[2,256,768]{2,0,1:T(2,128)(2,1)}) %all-reduce.3.cloned.1.call-update) | async-done | bytes 786448
  196.5 1.1 constant_dynamic-slice_fusion
  197.5 1.7 add_convert_fusion
  (30 shorter events, 0.1 us)
Async XLA Ops:
  6.5 139.9 %copy-start = (bf16[768,768]{1,0:T(8,128)(2,1)S(1)}, bf16[768,768]{1,0:T(8,128)(2,1)}, u32[]{:S(2)}) copy-start(bf16[768,768]{1,0:T(8,128)(2,1)} %param.22) | copy-start | bytes 3538948
  14.7 6.8 %copy-start.4 = (bf16[256,192]{0,1:T(8,128)(2,1)S(1)}, bf16[256,192]{0,1:T(8,128)(2,1)}, u32[]{:S(2)}) copy-start(bf16[256,192]{0,1:T(8,128)(2,1)} %param.17) | copy-start | bytes 294916
  14.7 7.5 %copy-start.5 = (bf16[768]{0:T(1024)(128)(2,1)S(1)}, bf16[768]{0:T(1024)(128)(2,1)}, u32[]{:S(2)}) copy-start(bf16[768]{0:T(1024)(128)(2,1)} %param.20) | copy-start | bytes 4612
  16.2 17.8 %all-to-all-start = ((bf16[8,2,24576]{2,1,0:T(2,128)(2,1)}), bf16[8,2,24576]{2,1,0:T(2,128)(2,1)S(1)}, u32[]{:S(2)}, u32[]{:S(2)}) async-start(bf16[8,2,24576]{2,1,0:T(2,128)(2,1)} %reshape.150), calls=%async_computation | async-start | bytes 1572864 | tf_op jit(solution)/shard_map/all_to_all | solution.py:50
  21.4 120.6 %all-gather.3.cloned.1.call-start = ((), (), s32[]{:S(2)}) async-start(), calls=%async_computation.1 | async-start | bytes 3932160 | tf_op jit(solution)/shard_map/all_gather | solution.py:14
  35.7 19.0 %copy-start.1 = (f32[256,192]{0,1:T(8,128)S(1)}, f32[256,192]{0,1:T(8,128)}, u32[]{:S(2)}) copy-start(f32[256,192]{0,1:T(8,128)} %convert_element_type.53) | copy-start | bytes 589828
  35.7 19.0 %copy-start.3 = (bf16[768,192]{0,1:T(8,128)(2,1)S(1)}, bf16[768,192]{0,1:T(8,128)(2,1)}, u32[]{:S(2)}) copy-start(bf16[768,192]{0,1:T(8,128)(2,1)} %param.16) | copy-start | bytes 884740
  73.3 1.2 copy-start.8
  76.0 1.0 copy-start.2
  76.9 1.6 copy-start.6
  78.3 118.2 %all-reduce.3.cloned.1.call-start = ((), (), s32[]{:S(2)}) async-start(), calls=%async_computation.2 | async-start | bytes 1572864
  146.4 1.3 copy-start.7
  152.1 1.8 copy-start.9
Sparse Core Ops, SparseCore 0:
  78.4 63.6 all-gather.2
  154.0 42.4 all-reduce.2
